TPU v7x, 32 devices: a whole 2x2x4 slice. The times are simulated.
32 devices in a mesh: lat: 4 (over y, x), lon: 4 (over z), mem: 2 (over core).
Axes of the slice: x: 2, y: 2, z: 4, core: 2. Of those that a mesh axis runs over, the one named last changes fastest.
Arguments:
- anomalies: bfloat16 [24, 4, 1440, 512], P('mem', None, 'lon', 'lat'), may hold values from -6 to 6
- taper: float32 [4, 1440, 512], P('lon', 'lat'), may hold values from 0.5 to 8
- obs_row: int32 [256, 512], P('lat', 'lon'), may hold values from 0 to 511, as said below
- obs_col: int32 [256, 512], P('lat', 'lon'), may hold values from 0 to 1439, as said below
- obs_level: int32 [256, 512], P('lat', 'lon'), may hold values from 0 to 3
- obs_value: float32 [256, 512], P('lat', 'lon'), may hold values from -18 to 18
Outputs:
- increment: float32 [4, 1440, 512], P(None, 'lon', 'lat')
Inputs may be any that keep to these rules, and one draw needn't show every extreme that they name: `obs_row`: the entry in row i lies in latitude rows (i // 64) * 128 to (i // 64 + 1) * 128 - 1, drawn evenly there. `obs_col`: the entry in column j lies in longitude columns (j // 128) * 360 to (j // 128 + 1) * 360 - 1, drawn evenly there.
All inputs are finite; a program needn't handle non-finite values.
Results may differ from a plain program's by a relative error of at most 0.0066.
Values may be sent and summed in bfloat16 or wider, within the bound.
A program may use at most 128 MiB of HBM per device.

v0:
```python
import math
import jax
import jax.numpy as jnp
from jax import lax
from jax.sharding import PartitionSpec as P


def lon_basis(length):
    grid_idx = jnp.arange(length, dtype=jnp.int32)[:, None]
    coef_idx = jnp.arange(length, dtype=jnp.int32)[None, :]
    nyquist = length // 2
    wavenum = jnp.where(coef_idx <= nyquist, coef_idx, coef_idx - nyquist)
    phase_idx = grid_idx * wavenum % length
    angles = phase_idx.astype(jnp.float32) * (2.0 * math.pi / length)
    scales = jnp.where(
        (coef_idx == 0) | (coef_idx == nyquist), 1.0 / math.sqrt(length), math.sqrt(2.0 / length)
    )
    basis = jnp.where(coef_idx <= nyquist, jnp.cos(angles), jnp.sin(angles)) * scales
    return basis.astype(jnp.bfloat16)


def lat_basis(length):
    grid_idx = jnp.arange(length, dtype=jnp.int32)[:, None]
    mode_idx = jnp.arange(length, dtype=jnp.int32)[None, :]
    phase_idx = mode_idx * (2 * grid_idx + 1) % (4 * length)
    angles = phase_idx.astype(jnp.float32) * (math.pi / (2.0 * length))
    scales = jnp.where(mode_idx == 0, 1.0 / math.sqrt(length), math.sqrt(2.0 / length))
    return (jnp.cos(angles) * scales).astype(jnp.bfloat16)


def spread_observations(cell_keys, row_local, obs_value, slot_count, row_count):
    obs_count = cell_keys.size
    block_rows = min(obs_count, 2048)
    turn_count = obs_count // block_rows
    key_blocks = cell_keys.reshape(turn_count, block_rows)
    row_blocks = row_local.reshape(turn_count, block_rows)
    value_blocks = obs_value.reshape(turn_count, block_rows)
    slot_ids = jnp.arange(slot_count, dtype=jnp.int32)
    row_ids = jnp.arange(row_count, dtype=jnp.int32)

    def add_block(running, obs_block):
        key_part, row_part, value_part = obs_block
        left_hot = (key_part[:, None] == slot_ids[None, :]).astype(jnp.bfloat16)
        high_part = value_part.astype(jnp.bfloat16)
        remainder = value_part - high_part.astype(jnp.float32)
        middle_part = remainder.astype(jnp.bfloat16)
        low_part = (remainder - middle_part.astype(jnp.float32)).astype(jnp.bfloat16)
        pieces = jnp.stack([high_part, middle_part, low_part], axis=1)
        row_hits = (row_part[:, None] == row_ids[None, :]).astype(jnp.bfloat16)
        weighted_rows = (pieces[:, :, None] * row_hits[:, None, :]).reshape(
            block_rows, 3 * row_count
        )
        added = jnp.einsum("ok,oz->kz", left_hot, weighted_rows, preferred_element_type=jnp.float32)
        return (running + added, None)

    start_sum = jnp.zeros((slot_count, 3 * row_count), jnp.float32)
    running, _ = lax.scan(add_block, start_sum, (key_blocks, row_blocks, value_blocks))
    return jnp.sum(running.reshape(slot_count, 3, row_count), axis=1)


def local(anomalies, taper, obs_row, obs_col, obs_level, obs_value):
    member_count, level_count, col_count, row_count = anomalies.shape
    lon_total = col_count * lax.axis_size("lon")
    lat_total = row_count * lax.axis_size("lat")
    row_start = lax.axis_index("lat") * row_count
    col_start = lax.axis_index("lon") * col_count
    cell_keys = (obs_level * col_count + (obs_col - col_start)).reshape(-1)
    row_local = (obs_row - row_start).reshape(-1)
    innovation = spread_observations(
        cell_keys, row_local, obs_value.reshape(-1), level_count * col_count, row_count
    )
    innovation = innovation.reshape(level_count, col_count, row_count).astype(jnp.bfloat16)
    lon_table = lon_basis(lon_total)
    lat_table = lat_basis(lat_total)
    ensemble = member_count * lax.axis_size("mem")
    fields, innov_cols = (
        lax.all_to_all(anomalies, "lon", split_axis=1, concat_axis=2, tiled=True),
        lax.all_to_all(innovation[None], "lon", split_axis=1, concat_axis=2, tiled=True),
    )
    zonal_coef = jnp.einsum(
        "alxy,xk->alky", fields * innov_cols, lon_table, preferred_element_type=jnp.float32
    ).astype(jnp.bfloat16)
    modal_zonal_coef = lax.all_to_all(zonal_coef, "lat", split_axis=2, concat_axis=3, tiled=True)
    spectrum = jnp.einsum(
        "alky,yn->alkn", modal_zonal_coef, lat_table, preferred_element_type=jnp.float32
    )
    tapered = (spectrum * taper[None]).astype(jnp.bfloat16)
    filtered = jnp.einsum(
        "alkn,yn->alky", tapered, lat_table, preferred_element_type=jnp.float32
    ).astype(jnp.bfloat16)
    inverse = lax.all_to_all(filtered, "lat", split_axis=3, concat_axis=2, tiled=True)
    localized = jnp.einsum("alky,xk->alxy", inverse, lon_table, preferred_element_type=jnp.float32)
    local_sum = jnp.sum(fields.astype(jnp.float32) * localized, axis=0)
    merged = lax.psum(local_sum, "mem")
    summed = lax.all_to_all(merged, "lon", split_axis=1, concat_axis=0, tiled=True)
    return summed / (ensemble - 1)


def solution(mesh):
    in_specs = (
        P("mem", None, "lon", "lat"),
        P("lon", "lat", None),
        P("lat", "lon"),
        P("lat", "lon"),
        P("lat", "lon"),
        P("lat", "lon"),
    )
    out_specs = P(None, "lon", "lat")
    return jax.shard_map(local, mesh=mesh, in_specs=in_specs, out_specs=out_specs, check_vma=False)
```

profile of v0, /device:TPU:0, one launch (start us, length us, event | category | flops | bytes accessed | tf_op | source)
XLA Modules:
  0.0 481.3 jit_solution(4805282629353373172)
XLA Ops:
  6.5 4.6 copy.33
  11.1 6.5 %all-to-all-start = ((bf16[12,4,360,128]{3,2,0,1:T(8,128)(2,1)}), bf16[12,4,360,128]{3,2,0,1:T(8,128)(2,1)}, u32[]{:S(2)}, u32[]{:S(2)}) async-start(bf16[12,4,360,128]{3,2,0,1:T(8,128)(2,1)} %copy.33), calls=%async_computation | async-start | bytes 8847360 | tf_op jit(solution)/shard_map/all_to_all | solution.py:77
  17.7 27.3 %while.11 = (s32[]{:T(128)}, f32[1440,384]{1,0:T(8,128)}, s32[4,2048]{1,0:T(4,128)S(1)}, f32[4,2048]{1,0:T(4,128)S(1)}, s32[4,2048]{1,0:T(4,128)S(1)}, /*index=5*/s32[]{:T(128)}, s32[]{:T(128)}) while((s32[]{:T(128)}, f32[1440,384]{1,0:T(8,128)}, s32[4,2048]{1,0:T(4,128)S(1)}, f32[4,2048]{1,0:T(4,128)S(1)}, ...), condition=%wide.region_1.2_spmd.clone, body=%wide.region_0.1_spmd.clone.sunk | while | flops 2273290240 | bytes 8728675 | solution.py:57
  18.1 5.2 %fusion.95 = f32[1440,384]{1,0:T(8,128)} fusion(bf16[2048,384]{0,1:T(8,128)(2,1)S(1)} %bitcast.84, s32[2048]{0:T(1024)S(1)} %bitcast.91, f32[1440,384]{1,0:T(8,128)} %get-tuple-element.126, pred[]{:T(512)S(6)} %compare.4), kind=kOutput, calls=%fused_computation.6.clone.1 | convolution fusion | flops 2271928320 | bytes 6004737 | tf_op jit(solution)/shard_map/while/body/eval_jaxpr/ok,oz->kz/dot_general | solution.py:53
  23.7 6.8 %fusion.95 = f32[1440,384]{1,0:T(8,128)} fusion(bf16[2048,384]{0,1:T(8,128)(2,1)S(1)} %bitcast.84, s32[2048]{0:T(1024)S(1)} %bitcast.91, f32[1440,384]{1,0:T(8,128)} %get-tuple-element.126, pred[]{:T(512)S(6)} %compare.4), kind=kOutput, calls=%fused_computation.6.clone.1 | convolution fusion | flops 2271928320 | bytes 6004737 | tf_op jit(solution)/shard_map/while/body/eval_jaxpr/ok,oz->kz/dot_general | solution.py:53
  30.9 6.9 %fusion.95 = f32[1440,384]{1,0:T(8,128)} fusion(bf16[2048,384]{0,1:T(8,128)(2,1)S(1)} %bitcast.84, s32[2048]{0:T(1024)S(1)} %bitcast.91, f32[1440,384]{1,0:T(8,128)} %get-tuple-element.126, pred[]{:T(512)S(6)} %compare.4), kind=kOutput, calls=%fused_computation.6.clone.1 | convolution fusion | flops 2271928320 | bytes 6004737 | tf_op jit(solution)/shard_map/while/body/eval_jaxpr/ok,oz->kz/dot_general | solution.py:53
  38.2 6.8 %fusion.95 = f32[1440,384]{1,0:T(8,128)} fusion(bf16[2048,384]{0,1:T(8,128)(2,1)S(1)} %bitcast.84, s32[2048]{0:T(1024)S(1)} %bitcast.91, f32[1440,384]{1,0:T(8,128)} %get-tuple-element.126, pred[]{:T(512)S(6)} %compare.4), kind=kOutput, calls=%fused_computation.6.clone.1 | convolution fusion | flops 2271928320 | bytes 6004737 | tf_op jit(solution)/shard_map/while/body/eval_jaxpr/ok,oz->kz/dot_general | solution.py:53
  45.0 2.0 copy.36
  47.0 0.2 reduce_sum.20
  47.3 0.9 copy.37
  48.2 67.8 %all-to-all-done = bf16[12,4,360,128]{3,2,0,1:T(8,128)(2,1)} async-done(((bf16[12,4,360,128]{3,2,0,1:T(8,128)(2,1)}), bf16[12,4,360,128]{3,2,0,1:T(8,128)(2,1)}, u32[]{:S(2)}, u32[]{:S(2)}) %all-to-all-start) | async-done | bytes 4423712 | tf_op jit(solution)/shard_map/all_to_all | solution.py:77
  116.0 3.9 all-to-all-start.1
  119.9 39.0 %fusion.84 = bf16[1440,1440,1]{1,0,2:T(8,128)(2,1)} fusion(f32[1440]{0:T(1024)S(1)} %fusion.58, s32[1440]{0:T(1024)S(1)} %add_select_fusion.2, pred[1440]{0:T(1024)(128)(4,1)S(1)} %iota_compare_fusion.4), kind=kLoop, calls=%fused_computation.29.clone.clone.clone.clone.1 | loop fusion | flops 24883200 | bytes 4160160 | tf_op jit(solution)/shard_map/alxy,xk->alky/dot_general | solution.py:80
  158.9 4.7 copy.35
  163.6 2.9 bitcast_multiply_fusion.1
  166.5 0.7 copy-done.5
  167.2 7.6 %fusion.28 = bf16[12,1,1440,128]{3,2,0,1:T(8,128)(2,1)S(1)} fusion(bf16[12,1440,128]{2,1,0:T(8,128)(2,1)S(1)} %bitcast_multiply_fusion.1, bf16[1440,1440,1]{1,0,2:T(8,128)(2,1)S(1)} %copy-done.5), kind=kOutput, calls=%fused_computation.39 | convolution fusion | flops 6372311040 | bytes 12994560 | tf_op jit(solution)/shard_map/alxy,xk->alky/dot_general | solution.py:80
  174.8 12.3 %copy.40 = bf16[12,1,1440,128]{3,0,1,2:T(8,128)(2,1)} copy(bf16[12,1,1440,128]{3,2,0,1:T(8,128)(2,1)S(1)} %fusion.28) | data formatting | bytes 8847360 | tf_op jit(solution)/shard_map/convert_element_type | solution.py:82
  187.1 5.2 %all-to-all-start.2 = ((bf16[12,1,1440,128]{3,0,1,2:T(8,128)(2,1)}), bf16[12,1,1440,128]{3,0,1,2:T(8,128)(2,1)}, u32[]{:S(2)}, u32[]{:S(2)}) async-start(bf16[12,1,1440,128]{3,0,1,2:T(8,128)(2,1)} %copy.40), calls=%async_computation.2 | async-start | bytes 11796480 | tf_op jit(solution)/shard_map/all_to_all | solution.py:83
  192.3 65.0 %all-to-all-done.2 = bf16[12,1,1440,128]{3,0,1,2:T(8,128)(2,1)} async-done(((bf16[12,1,1440,128]{3,0,1,2:T(8,128)(2,1)}), bf16[12,1,1440,128]{3,0,1,2:T(8,128)(2,1)}, u32[]{:S(2)}, u32[]{:S(2)}) %all-to-all-start.2) | async-done | bytes 4423712 | tf_op jit(solution)/shard_map/all_to_all | solution.py:83
  257.3 8.2 %copy.47 = bf16[12,1,4,360,128]{4,2,3,0,1:T(4,128)(2,1)} copy(bf16[12,1,4,360,128]{4,0,3,2,1:T(8,128)(2,1)} %bitcast.10) | data formatting | bytes 8847360 | tf_op jit(solution)/shard_map/all_to_all | solution.py:83
  265.5 8.6 %reshape.193 = bf16[12,360,512]{2,1,0:T(8,128)(2,1)} reshape(bf16[12,1,360,4,128]{4,3,2,0,1:T(4,128)(2,1)} %bitcast.85) | data formatting | bytes 8847360 | tf_op jit(solution)/shard_map/reshape.13
  274.1 16.1 %convert_bitcast_fusion = bf16[12,1,360,512]{3,2,0,1:T(8,128)(2,1)} fusion(f32[360,512]{1,0:T(8,128)S(1)} %bitcast.92, bf16[12,360,512]{2,1,0:T(8,128)(2,1)} %reshape.193, f32[512]{0:T(512)S(1)} %fusion.59, s32[512]{0:T(512)S(1)} %multiply_add_fusion), kind=kOutput, calls=%fused_computation.33 | convolution fusion | flops 4544872448 | bytes 9588736 | tf_op jit(solution)/shard_map/alkn,yn->alky/dot_general | solution.py:88
  290.2 8.9 %copy.42 = bf16[12,1,360,512]{2,0,1,3:T(8,128)(2,1)} copy(bf16[12,1,360,512]{3,2,0,1:T(8,128)(2,1)} %convert_bitcast_fusion) | data formatting | bytes 8847360 | tf_op jit(solution)/shard_map/convert_element_type | solution.py:90
  299.2 5.2 %all-to-all-start.3 = ((bf16[12,1,360,512]{2,0,1,3:T(8,128)(2,1)}), bf16[12,1,360,512]{2,0,1,3:T(8,128)(2,1)}, u32[]{:S(2)}, u32[]{:S(2)}) async-start(bf16[12,1,360,512]{2,0,1,3:T(8,128)(2,1)} %copy.42), calls=%async_computation.3 | async-start | bytes 12582912 | tf_op jit(solution)/shard_map/all_to_all | solution.py:91
  304.5 6.4 %copy.34 = f32[12,4,360,128]{3,2,1,0:T(8,128)} copy(bf16[12,4,360,128]{3,2,0,1:T(8,128)(2,1)} %all-to-all-done) | data formatting | bytes 13271040 | tf_op jit(solution)/shard_map/convert_element_type | solution.py:93
  310.9 62.9 %all-to-all-done.3 = bf16[12,1,360,512]{2,0,1,3:T(8,128)(2,1)} async-done(((bf16[12,1,360,512]{2,0,1,3:T(8,128)(2,1)}), bf16[12,1,360,512]{2,0,1,3:T(8,128)(2,1)}, u32[]{:S(2)}, u32[]{:S(2)}) %all-to-all-start.3) | async-done | bytes 4423712 | tf_op jit(solution)/shard_map/all_to_all | solution.py:91
  373.8 8.8 %copy.43 = bf16[12,1,360,4,128]{4,2,3,0,1:T(8,128)(2,1)} copy(bf16[12,1,360,4,128]{2,0,4,3,1:T(8,128)(2,1)} %bitcast.15) | data formatting | bytes 8847360 | tf_op jit(solution)/shard_map/all_to_all | solution.py:91
  382.5 46.6 %fusion.15 = f32[1440,128]{1,0:T(8,128)} fusion(f32[12,4,360,128]{3,2,1,0:T(8,128)} %copy.34, bf16[12,1440,128]{2,1,0:T(8,128)(2,1)} %bitcast.87, f32[1440]{0:T(1024)S(1)} %fusion.58, s32[1440]{0:T(1024)S(1)} %add_select_fusion.2, pred[1440]{0:T(1024)(128)(4,1)S(1)} %iota_compare_fusion.4), kind=kOutput, calls=%fused_computation.21 | convolution fusion | flops 6399221760 | bytes 14021280 | tf_op jit(solution)/shard_map/alky,xk->alxy/dot_general | solution.py:92
  429.1 19.2 %all-reduce.2.cloned.1.call-done = f32[1,1440,128]{2,0,1:T(1,128)} async-done(((f32[1,1440,128]{2,0,1:T(1,128)}), f32[1,1440,128]{2,0,1:T(1,128)}) %all-reduce.2.cloned.1.call-update) | async-done | bytes 737296 | tf_op jit(solution)/shard_map/psum | solution.py:94
  448.3 24.4 %all_to_all.60 = f32[1,1440,128]{2,0,1:T(1,128)S(1)} all-to-all(f32[1,1440,128]{2,0,1:T(1,128)} %all-reduce.2.cloned.1.call-done), channel_id=1, replica_groups=mesh['lat'=4,'lon'=4,'mem'=2] {'lon'}, dimensions={1} | all-to-all | bytes 1474560 | tf_op jit(solution)/shard_map/all_to_all | solution.py:95
  472.7 1.5 broadcast_multiply_fusion.1
  (49 shorter events, 1.5 us)
Async XLA Ops:
  11.1 6.5 %copy-start.2 = (s32[64,128]{1,0:T(8,128)S(1)}, s32[64,128]{1,0:T(8,128)}, u32[]{:S(2)}) copy-start(s32[64,128]{1,0:T(8,128)} %param.10) | copy-start | bytes 98308
  11.1 6.5 %copy-start = (s32[64,128]{1,0:T(8,128)S(1)}, s32[64,128]{1,0:T(8,128)}, u32[]{:S(2)}) copy-start(s32[64,128]{1,0:T(8,128)} %param.11) | copy-start | bytes 98308
  11.1 6.5 %copy-start.1 = (s32[64,128]{1,0:T(8,128)S(1)}, s32[64,128]{1,0:T(8,128)}, u32[]{:S(2)}) copy-start(s32[64,128]{1,0:T(8,128)} %param.12) | copy-start | bytes 98308
  11.1 6.6 %copy-start.3 = (f32[64,128]{1,0:T(8,128)S(1)}, f32[64,128]{1,0:T(8,128)}, u32[]{:S(2)}) copy-start(f32[64,128]{1,0:T(8,128)} %param.13) | copy-start | bytes 98308
  11.1 104.9 %all-to-all-start = ((bf16[12,4,360,128]{3,2,0,1:T(8,128)(2,1)}), bf16[12,4,360,128]{3,2,0,1:T(8,128)(2,1)}, u32[]{:S(2)}, u32[]{:S(2)}) async-start(bf16[12,4,360,128]{3,2,0,1:T(8,128)(2,1)} %copy.33), calls=%async_computation | async-start | bytes 8847360 | tf_op jit(solution)/shard_map/all_to_all | solution.py:77
  116.0 47.6 %all-to-all-start.1 = ((bf16[1,4,360,128]{3,2,0,1:T(8,128)(2,1)}), bf16[1,4,360,128]{3,2,0,1:T(8,128)(2,1)S(1)}, u32[]{:S(2)}, u32[]{:S(2)}) async-start(bf16[1,4,360,128]{3,2,0,1:T(8,128)(2,1)} %bitcast.6), calls=%async_computation.1 | async-start | bytes 737280 | tf_op jit(solution)/shard_map/all_to_all | solution.py:78
  163.6 3.6 copy-start.5
  187.1 70.2 %all-to-all-start.2 = ((bf16[12,1,1440,128]{3,0,1,2:T(8,128)(2,1)}), bf16[12,1,1440,128]{3,0,1,2:T(8,128)(2,1)}, u32[]{:S(2)}, u32[]{:S(2)}) async-start(bf16[12,1,1440,128]{3,0,1,2:T(8,128)(2,1)} %copy.40), calls=%async_computation.2 | async-start | bytes 11796480 | tf_op jit(solution)/shard_map/all_to_all | solution.py:83
  265.5 8.6 %copy-start.4 = (f32[1,360,512]{2,1,0:T(8,128)S(1)}, f32[1,360,512]{2,1,0:T(8,128)}, u32[]{:S(2)}) copy-start(f32[1,360,512]{2,1,0:T(8,128)} %param.9) | copy-start | bytes 2211844
  299.2 74.6 %all-to-all-start.3 = ((bf16[12,1,360,512]{2,0,1,3:T(8,128)(2,1)}), bf16[12,1,360,512]{2,0,1,3:T(8,128)(2,1)}, u32[]{:S(2)}, u32[]{:S(2)}) async-start(bf16[12,1,360,512]{2,0,1,3:T(8,128)(2,1)} %copy.42), calls=%async_computation.3 | async-start | bytes 12582912 | tf_op jit(solution)/shard_map/all_to_all | solution.py:91
  304.4 143.9 %all-reduce.2.cloned.1.call-start = ((), (), s32[]{:S(2)}) async-start(), calls=%async_computation.5 | async-start | bytes 1474560 | tf_op jit(solution)/shard_map/psum | solution.py:94
Sparse Core Ops, SparseCore 0:
  429.2 19.0 all-reduce.1
where the time goes:
time: 487 us; the launch traced here: 481 us
  waiting for transfers between devices  215 us (44%)
  matrix products  96 us (20%)
  local copies, waits for them, and re-layouts  66.3 us (14%)
  other arithmetic  44.8 us (9%)
  blocking collectives  24.4 us (5%)
  starting transfers between devices  20.9 us (4%)
  between operations  13.8 us (3%)
    all_to_all x1, waiting for transfers between devices, local(): lax.all_to_all(anomalies, 'lon', split_axis=1, concat_axis=2, tiled=True)  67.8 us
    all_to_all x1, waiting for transfers between devices, local(): lax.all_to_all(zonal_coef, 'lat', split_axis=2, concat_axis=3, tiled=True)  65 us
    all_to_all x1, waiting for transfers between devices, local(): lax.all_to_all(filtered, 'lat', split_axis=3, concat_axis=2, tiled=True)  62.9 us
    dot_general x1, matrix products, local(): jnp.einsum('alky,xk->alxy', inverse, lon_table, preferred_element_type=jn...  46.6 us
    dot_general x1, other arithmetic, local(): jnp.einsum('alxy,xk->alky', fields * innov_cols, lon_table, preferred_ele...  39 us
    dot_general x4, matrix products, add_block(): jnp.einsum('ok,oz->kz', left_hot, weighted_rows, preferred_element_type=j...  25.7 us
    all_to_all x1, blocking collectives, local(): lax.all_to_all(merged, 'lon', split_axis=1, concat_axis=0, tiled=True)  24.4 us
    psum x1, waiting for transfers between devices, local(): merged = lax.psum(local_sum, 'mem')  19.2 us
  transfers between devices with their start and end apart: 5, of which 4 were waited for; matrix products, arithmetic and copies ran while one was open for 17% of the time, Pallas kernels for 0%

commit v1 on v0

--- a/solution.py
+++ b/solution.py
@@ -88,7 +88,10 @@
     filtered = jnp.einsum(
         "alkn,yn->alky", tapered, lat_table, preferred_element_type=jnp.float32
     ).astype(jnp.bfloat16)
-    inverse = lax.all_to_all(filtered, "lat", split_axis=3, concat_axis=2, tiled=True)
+    inverse = jnp.concatenate(
+        lax.all_to_all(jnp.stack(jnp.split(filtered, lax.axis_size("lat"), axis=3)), "lat", 0, 0),
+        axis=2,
+    )
     localized = jnp.einsum("alky,xk->alxy", inverse, lon_table, preferred_element_type=jnp.float32)
     local_sum = jnp.sum(fields.astype(jnp.float32) * localized, axis=0)
     merged = lax.psum(local_sum, "mem")

time: 487 us -> 456 us (0.936)
  waiting for transfers between devices: 215 us -> 195 us
  local copies, waits for them, and re-layouts: 66.3 us -> 56.2 us
    all_to_all x1, waiting for transfers between devices: 62.9 us -> 42.7 us  [local(): lax.all_to_all(jnp.stack(jnp.split(filtered, lax.axis_size('lat'), axis=3...]
    convert_element_type x1 -> x0, local copies, waits for them, and re-layouts: 8.94 us -> none  [local(): filtered = jnp.einsum('alkn,yn->alky', tapered, lat_table, preferred_elem...]
    all_to_all x1 -> x0, local copies, waits for them, and re-layouts: 8.75 us -> none  [local(): lax.all_to_all(filtered, 'lat', split_axis=3, concat_axis=2, tiled=True)]
    another operation x1 -> x2, local copies, waits for them, and re-layouts: 8.6 us -> 11.1 us
  transfers between devices with their start and end apart: 5 -> 5, of which waited for: 4 -> 4; matrix products, arithmetic and copies ran while one was open for 17% -> 18% of each run, Pallas kernels for 0% -> 0%
where the time goes in v1:
time: 456 us; the launch traced here: 451 us
  waiting for transfers between devices  195 us (43%)
  matrix products  93.3 us (20%)
  local copies, waits for them, and re-layouts  56.2 us (12%)
  other arithmetic  47.1 us (10%)
  blocking collectives  24.4 us (5%)
  starting transfers between devices  20.9 us (5%)
  between operations  13.8 us (3%)
    all_to_all x1, waiting for transfers between devices, local(): lax.all_to_all(anomalies, 'lon', split_axis=1, concat_axis=2, tiled=True)  67.9 us
    all_to_all x1, waiting for transfers between devices, local(): lax.all_to_all(zonal_coef, 'lat', split_axis=2, concat_axis=3, tiled=True)  65.1 us
    dot_general x1, matrix products, local(): jnp.einsum('alky,xk->alxy', inverse, lon_table, preferred_element_type=jn...  43.9 us
    all_to_all x1, waiting for transfers between devices, local(): lax.all_to_all(jnp.stack(jnp.split(filtered, lax.axis_size('lat'), axis=3...  42.7 us
    dot_general x1, other arithmetic, local(): jnp.einsum('alxy,xk->alky', fields * innov_cols, lon_table, preferred_ele...  39 us
    dot_general x4, matrix products, add_block(): jnp.einsum('ok,oz->kz', left_hot, weighted_rows, preferred_element_type=j...  25.6 us
    all_to_all x1, blocking collectives, local(): lax.all_to_all(merged, 'lon', split_axis=1, concat_axis=0, tiled=True)  24.4 us
    psum x1, waiting for transfers between devices, local(): merged = lax.psum(local_sum, 'mem')  19.2 us
  transfers between devices with their start and end apart: 5, of which 4 were waited for; matrix products, arithmetic and copies ran while one was open for 18% of the time, Pallas kernels for 0%

profile of v1, /device:TPU:0, one launch (start us, length us, event | category | flops | bytes accessed | tf_op | source)
XLA Modules:
  0.0 450.8 jit_solution(1033809555501160238)
XLA Ops:
  6.5 4.7 %copy.30 = bf16[12,4,360,128]{3,2,0,1:T(8,128)(2,1)} copy(bf16[12,4,360,128]{3,2,1,0:T(8,128)(2,1)} %param.8) | data formatting | bytes 8847360 | tf_op args[0]
  11.2 6.5 %all-to-all-start = ((bf16[12,4,360,128]{3,2,0,1:T(8,128)(2,1)}), bf16[12,4,360,128]{3,2,0,1:T(8,128)(2,1)}, u32[]{:S(2)}, u32[]{:S(2)}) async-start(bf16[12,4,360,128]{3,2,0,1:T(8,128)(2,1)} %copy.30), calls=%async_computation | async-start | bytes 8847360 | tf_op jit(solution)/shard_map/all_to_all | solution.py:77
  17.8 27.1 %while.11 = (s32[]{:T(128)}, f32[1440,384]{1,0:T(8,128)}, s32[4,2048]{1,0:T(4,128)S(1)}, f32[4,2048]{1,0:T(4,128)S(1)}, s32[4,2048]{1,0:T(4,128)S(1)}, /*index=5*/s32[]{:T(128)}, s32[]{:T(128)}) while((s32[]{:T(128)}, f32[1440,384]{1,0:T(8,128)}, s32[4,2048]{1,0:T(4,128)S(1)}, f32[4,2048]{1,0:T(4,128)S(1)}, ...), condition=%wide.region_1.2_spmd.clone, body=%wide.region_0.1_spmd.clone.sunk | while | flops 2273290240 | bytes 8728675 | solution.py:57
  18.2 5.2 %fusion.95 = f32[1440,384]{1,0:T(8,128)} fusion(bf16[2048,384]{0,1:T(8,128)(2,1)S(1)} %bitcast.90, s32[2048]{0:T(1024)S(1)} %bitcast.97, f32[1440,384]{1,0:T(8,128)} %get-tuple-element.130, pred[]{:T(512)S(6)} %compare.4), kind=kOutput, calls=%fused_computation.6.clone.1 | convolution fusion | flops 2271928320 | bytes 6004737 | tf_op jit(solution)/shard_map/while/body/eval_jaxpr/ok,oz->kz/dot_general | solution.py:53
  23.8 6.8 %fusion.95 = f32[1440,384]{1,0:T(8,128)} fusion(bf16[2048,384]{0,1:T(8,128)(2,1)S(1)} %bitcast.90, s32[2048]{0:T(1024)S(1)} %bitcast.97, f32[1440,384]{1,0:T(8,128)} %get-tuple-element.130, pred[]{:T(512)S(6)} %compare.4), kind=kOutput, calls=%fused_computation.6.clone.1 | convolution fusion | flops 2271928320 | bytes 6004737 | tf_op jit(solution)/shard_map/while/body/eval_jaxpr/ok,oz->kz/dot_general | solution.py:53
  31.0 6.8 %fusion.95 = f32[1440,384]{1,0:T(8,128)} fusion(bf16[2048,384]{0,1:T(8,128)(2,1)S(1)} %bitcast.90, s32[2048]{0:T(1024)S(1)} %bitcast.97, f32[1440,384]{1,0:T(8,128)} %get-tuple-element.130, pred[]{:T(512)S(6)} %compare.4), kind=kOutput, calls=%fused_computation.6.clone.1 | convolution fusion | flops 2271928320 | bytes 6004737 | tf_op jit(solution)/shard_map/while/body/eval_jaxpr/ok,oz->kz/dot_general | solution.py:53
  38.1 6.8 %fusion.95 = f32[1440,384]{1,0:T(8,128)} fusion(bf16[2048,384]{0,1:T(8,128)(2,1)S(1)} %bitcast.90, s32[2048]{0:T(1024)S(1)} %bitcast.97, f32[1440,384]{1,0:T(8,128)} %get-tuple-element.130, pred[]{:T(512)S(6)} %compare.4), kind=kOutput, calls=%fused_computation.6.clone.1 | convolution fusion | flops 2271928320 | bytes 6004737 | tf_op jit(solution)/shard_map/while/body/eval_jaxpr/ok,oz->kz/dot_general | solution.py:53
  44.9 2.0 copy.33
  47.2 0.9 copy.34
  48.2 67.9 %all-to-all-done = bf16[12,4,360,128]{3,2,0,1:T(8,128)(2,1)} async-done(((bf16[12,4,360,128]{3,2,0,1:T(8,128)(2,1)}), bf16[12,4,360,128]{3,2,0,1:T(8,128)(2,1)}, u32[]{:S(2)}, u32[]{:S(2)}) %all-to-all-start) | async-done | bytes 4423712 | tf_op jit(solution)/shard_map/all_to_all | solution.py:77
  116.1 3.9 all-to-all-start.1
  120.0 39.0 %fusion.84 = bf16[1440,1440,1]{1,0,2:T(8,128)(2,1)} fusion(f32[1440]{0:T(1024)S(1)} %fusion.58, s32[1440]{0:T(1024)S(1)} %add_select_fusion.2, pred[1440]{0:T(1024)(128)(4,1)S(1)} %iota_compare_fusion.4), kind=kLoop, calls=%fused_computation.29.clone.clone.clone.clone.1 | loop fusion | flops 24883200 | bytes 4160160 | tf_op jit(solution)/shard_map/alxy,xk->alky/dot_general | solution.py:80
  159.0 4.7 %copy.32 = bf16[12,4,360,128]{3,2,1,0:T(8,128)(2,1)} copy(bf16[12,4,360,128]{3,2,0,1:T(8,128)(2,1)} %all-to-all-done) | data formatting | bytes 8847360 | tf_op jit(solution)/shard_map/all_to_all | solution.py:77
  163.7 2.9 bitcast_multiply_fusion.1
  167.3 7.6 %fusion.28 = bf16[12,1,1440,128]{3,2,0,1:T(8,128)(2,1)S(1)} fusion(bf16[12,1440,128]{2,1,0:T(8,128)(2,1)S(1)} %bitcast_multiply_fusion.1, bf16[1440,1440,1]{1,0,2:T(8,128)(2,1)S(1)} %copy-done.6), kind=kOutput, calls=%fused_computation.40 | convolution fusion | flops 6372311040 | bytes 12994560 | tf_op jit(solution)/shard_map/alxy,xk->alky/dot_general | solution.py:80
  174.9 12.3 %copy.37 = bf16[12,1,1440,128]{3,0,1,2:T(8,128)(2,1)} copy(bf16[12,1,1440,128]{3,2,0,1:T(8,128)(2,1)S(1)} %fusion.28) | data formatting | bytes 8847360 | tf_op jit(solution)/shard_map/convert_element_type | solution.py:82
  187.2 5.4 %all-to-all-start.2 = ((bf16[12,1,1440,128]{3,0,1,2:T(8,128)(2,1)}), bf16[12,1,1440,128]{3,0,1,2:T(8,128)(2,1)}, u32[]{:S(2)}, u32[]{:S(2)}) async-start(bf16[12,1,1440,128]{3,0,1,2:T(8,128)(2,1)} %copy.37), calls=%async_computation.2 | async-start | bytes 11796480 | tf_op jit(solution)/shard_map/all_to_all | solution.py:83
  192.7 65.1 %all-to-all-done.2 = bf16[12,1,1440,128]{3,0,1,2:T(8,128)(2,1)} async-done(((bf16[12,1,1440,128]{3,0,1,2:T(8,128)(2,1)}), bf16[12,1,1440,128]{3,0,1,2:T(8,128)(2,1)}, u32[]{:S(2)}, u32[]{:S(2)}) %all-to-all-start.2) | async-done | bytes 4423712 | tf_op jit(solution)/shard_map/all_to_all | solution.py:83
  257.8 8.2 %copy.43 = bf16[12,1,4,360,128]{4,2,3,0,1:T(4,128)(2,1)} copy(bf16[12,1,4,360,128]{4,0,3,2,1:T(8,128)(2,1)} %bitcast.10) | data formatting | bytes 8847360 | tf_op jit(solution)/shard_map/all_to_all | solution.py:83
  266.0 8.5 %reshape.197 = bf16[12,360,512]{2,1,0:T(8,128)(2,1)} reshape(bf16[12,1,360,4,128]{4,3,2,0,1:T(4,128)(2,1)} %bitcast.91) | data formatting | bytes 8847360 | tf_op jit(solution)/shard_map/reshape.15
  274.5 16.1 %convert_bitcast_fusion = bf16[12,1,360,512]{3,2,0,1:T(8,128)(2,1)} fusion(f32[360,512]{1,0:T(8,128)S(1)} %bitcast.98, bf16[12,360,512]{2,1,0:T(8,128)(2,1)} %reshape.197, f32[512]{0:T(512)S(1)} %fusion.59, s32[512]{0:T(512)S(1)} %multiply_add_fusion), kind=kOutput, calls=%fused_computation.34 | convolution fusion | flops 4544872448 | bytes 9588736 | tf_op jit(solution)/shard_map/alkn,yn->alky/dot_general | solution.py:88
  290.6 2.6 slice_bitcast_fusion.3
  293.2 2.4 pad_maximum_fusion.1
  295.5 4.9 %all-to-all-start.3 = ((bf16[4,12,1,360,128]{4,3,1,2,0:T(8,128)(2,1)}), bf16[4,12,1,360,128]{4,3,1,2,0:T(8,128)(2,1)}, u32[]{:S(2)}, u32[]{:S(2)}) async-start(bf16[4,12,1,360,128]{4,3,1,2,0:T(8,128)(2,1)} %pad_maximum_fusion.1), calls=%async_computation.3 | async-start | bytes 8847360 | tf_op jit(solution)/shard_map/all_to_all | solution.py:92
  300.7 6.5 %copy.31 = f32[12,4,360,128]{3,2,1,0:T(8,128)} copy(bf16[12,4,360,128]{3,2,0,1:T(8,128)(2,1)} %all-to-all-done) | data formatting | bytes 13271040 | tf_op jit(solution)/shard_map/convert_element_type | solution.py:96
  307.2 42.7 %all-to-all-done.3 = bf16[4,12,1,360,128]{4,3,1,2,0:T(8,128)(2,1)} async-done(((bf16[4,12,1,360,128]{4,3,1,2,0:T(8,128)(2,1)}), bf16[4,12,1,360,128]{4,3,1,2,0:T(8,128)(2,1)}, u32[]{:S(2)}, u32[]{:S(2)}) %all-to-all-start.3) | async-done | bytes 4423712 | tf_op jit(solution)/shard_map/all_to_all | solution.py:92
  349.8 2.7 copy.39
  352.5 2.1 copy-done
  354.7 43.9 %fusion.15 = f32[1440,128]{1,0:T(8,128)} fusion(f32[12,4,360,128]{3,2,1,0:T(8,128)S(1)} %copy-done, bf16[12,1440,128]{2,1,0:T(8,128)(2,1)S(1)} %bitcast.93, f32[1440]{0:T(1024)S(1)} %fusion.58, s32[1440]{0:T(1024)S(1)} %add_select_fusion.2, pred[1440]{0:T(1024)(128)(4,1)S(1)} %iota_compare_fusion.4), kind=kOutput, calls=%fused_computation.21 | convolution fusion | flops 6399221760 | bytes 14021280 | tf_op jit(solution)/shard_map/alky,xk->alxy/dot_general | solution.py:95
  398.6 19.2 %all-reduce.2.cloned.1.call-done = f32[1,1440,128]{2,0,1:T(1,128)} async-done(((f32[1,1440,128]{2,0,1:T(1,128)}), f32[1,1440,128]{2,0,1:T(1,128)}) %all-reduce.2.cloned.1.call-update) | async-done | bytes 737296 | tf_op jit(solution)/shard_map/psum | solution.py:97
  417.9 24.4 %all_to_all.50 = f32[1,1440,128]{2,0,1:T(1,128)S(1)} all-to-all(f32[1,1440,128]{2,0,1:T(1,128)} %all-reduce.2.cloned.1.call-done), channel_id=1, replica_groups=mesh['lat'=4,'lon'=4,'mem'=2] {'lon'}, dimensions={1} | all-to-all | bytes 1474560 | tf_op jit(solution)/shard_map/all_to_all | solution.py:98
  442.3 1.5 broadcast_multiply_fusion.1
  (52 shorter events, 2.6 us)
Async XLA Ops:
  11.2 6.5 %copy-start.3 = (s32[64,128]{1,0:T(8,128)S(1)}, s32[64,128]{1,0:T(8,128)}, u32[]{:S(2)}) copy-start(s32[64,128]{1,0:T(8,128)} %param.10) | copy-start | bytes 98308
  11.2 6.5 %copy-start.1 = (s32[64,128]{1,0:T(8,128)S(1)}, s32[64,128]{1,0:T(8,128)}, u32[]{:S(2)}) copy-start(s32[64,128]{1,0:T(8,128)} %param.11) | copy-start | bytes 98308
  11.2 6.5 %copy-start.2 = (s32[64,128]{1,0:T(8,128)S(1)}, s32[64,128]{1,0:T(8,128)}, u32[]{:S(2)}) copy-start(s32[64,128]{1,0:T(8,128)} %param.12) | copy-start | bytes 98308
  11.2 6.6 %copy-start.4 = (f32[64,128]{1,0:T(8,128)S(1)}, f32[64,128]{1,0:T(8,128)}, u32[]{:S(2)}) copy-start(f32[64,128]{1,0:T(8,128)} %param.13) | copy-start | bytes 98308
  11.2 104.9 %all-to-all-start = ((bf16[12,4,360,128]{3,2,0,1:T(8,128)(2,1)}), bf16[12,4,360,128]{3,2,0,1:T(8,128)(2,1)}, u32[]{:S(2)}, u32[]{:S(2)}) async-start(bf16[12,4,360,128]{3,2,0,1:T(8,128)(2,1)} %copy.30), calls=%async_computation | async-start | bytes 8847360 | tf_op jit(solution)/shard_map/all_to_all | solution.py:77
  116.1 47.6 %all-to-all-start.1 = ((bf16[1,4,360,128]{3,2,0,1:T(8,128)(2,1)}), bf16[1,4,360,128]{3,2,0,1:T(8,128)(2,1)S(1)}, u32[]{:S(2)}, u32[]{:S(2)}) async-start(bf16[1,4,360,128]{3,2,0,1:T(8,128)(2,1)} %bitcast.6), calls=%async_computation.1 | async-start | bytes 737280 | tf_op jit(solution)/shard_map/all_to_all | solution.py:78
  163.7 3.6 copy-start.6
  187.2 70.5 %all-to-all-start.2 = ((bf16[12,1,1440,128]{3,0,1,2:T(8,128)(2,1)}), bf16[12,1,1440,128]{3,0,1,2:T(8,128)(2,1)}, u32[]{:S(2)}, u32[]{:S(2)}) async-start(bf16[12,1,1440,128]{3,0,1,2:T(8,128)(2,1)} %copy.37), calls=%async_computation.2 | async-start | bytes 11796480 | tf_op jit(solution)/shard_map/all_to_all | solution.py:83
  266.0 8.5 %copy-start.5 = (f32[1,360,512]{2,1,0:T(8,128)S(1)}, f32[1,360,512]{2,1,0:T(8,128)}, u32[]{:S(2)}) copy-start(f32[1,360,512]{2,1,0:T(8,128)} %param.9) | copy-start | bytes 2211844
  295.5 54.3 %all-to-all-start.3 = ((bf16[4,12,1,360,128]{4,3,1,2,0:T(8,128)(2,1)}), bf16[4,12,1,360,128]{4,3,1,2,0:T(8,128)(2,1)}, u32[]{:S(2)}, u32[]{:S(2)}) async-start(bf16[4,12,1,360,128]{4,3,1,2,0:T(8,128)(2,1)} %pad_maximum_fusion.1), calls=%async_computation.3 | async-start | bytes 8847360 | tf_op jit(solution)/shard_map/all_to_all | solution.py:92
  300.4 117.4 %all-reduce.2.cloned.1.call-start = ((), (), s32[]{:S(2)}) async-start(), calls=%async_computation.5 | async-start | bytes 1474560 | tf_op jit(solution)/shard_map/psum | solution.py:97
  349.8 4.8 %copy-start = (f32[12,4,360,128]{3,2,1,0:T(8,128)S(1)}, f32[12,4,360,128]{3,2,1,0:T(8,128)}, u32[]{:S(2)}) copy-start(f32[12,4,360,128]{3,2,1,0:T(8,128)} %copy.31) | copy-start | bytes 26542084
Sparse Core Ops, SparseCore 0:
  398.8 19.0 all-reduce.1
